TPU v7x, 32 devices: a whole 2x2x4 slice. The times are simulated.
32 devices in a mesh: ctx: 4 (over x, core), head: 8 (over z, y).
Axes of the slice: x: 2, y: 2, z: 4, core: 2. Of those that a mesh axis runs over, the one named last changes fastest.
Arguments:
- layer_input: bfloat16 [1024, 8192], P('ctx'), may hold values from -6 to 6
- output_grad: bfloat16 [1024, 8192], P('ctx'), may hold values from -6 to 6
- routes: int32 [1024, 8], P('ctx'), may hold values from 0 to 31, all different within a row; in each aligned block of 256 rows (0 to 255, 256 to 511, ...) at most 128 rows name the same one
- route_gates: float32 [1024, 8], P('ctx'), may hold values from 0.05 to 0.3
- query_weight: bfloat16 [40, 8192, 128], P('head', 'ctx'), may hold values from -0.0625 to 0.0625
- output_weight: bfloat16 [40, 8192, 128], P('head', 'ctx'), may hold values from -0.0625 to 0.0625
- key_values: bfloat16 [8, 1024, 128], P('head', 'ctx'), may hold values from -96 to 96
Outputs:
- input_grad: bfloat16 [1024, 8192], P('ctx', 'head')
- keyvalue_grad: float32 [8, 1024, 128], P('head', 'ctx')
Inputs may be any that keep to these rules, and one draw needn't show every extreme that they name: `routes`: each row names 8 different experts; in the 256 rows of one ctx block no expert is named more than 128 times, and some expert reaches 128.
All inputs are finite; a program needn't handle non-finite values.
Results may differ from a plain program's by a relative error of at most 0.015.
The roundings to bfloat16 on the way count: a program that leaves them out, or rounds other values in their place, can miss the bound.
Values may be sent and summed in bfloat16 or wider, within the bound.
A program may use at most 128 MiB of HBM per device.

v0:
```python
import jax
import jax.numpy as jnp
from jax import lax
from jax.sharding import PartitionSpec as P

PRECISE = lax.Precision.HIGHEST


def swapped(value, axis, bit):
    mask = 2**bit
    pairs = [(source, source ^ mask) for source in range(lax.axis_size(axis))]
    return lax.ppermute(value, axis, pairs)


def slot_table(route_rows, first_id, expert_count, slot_count):
    expert_ids = first_id + jnp.arange(expert_count, dtype=jnp.int32)
    matches = route_rows[:, :, None] == expert_ids[None, None, :]
    member = jnp.any(matches, axis=1).astype(jnp.int32)
    placed = jnp.cumsum(member, axis=0) - 1
    slot_map = (placed.T[:, None, :] == jnp.arange(slot_count, dtype=jnp.int32)[None, :, None]) & (
        member.T[:, None, :] == 1
    )
    return slot_map.astype(jnp.float32)


def expert_gate(route_rows, gate_rows, first_id, expert_count):
    expert_ids = first_id + jnp.arange(expert_count, dtype=jnp.int32)
    matches = route_rows[:, :, None] == expert_ids[None, None, :]
    return jnp.sum(
        jnp.where(matches, gate_rows[:, :, None], jnp.zeros_like(gate_rows)[:, :, None]), axis=1
    )


def attend(queries, query_place, key_rows, value_rows, key_place, head_grads):
    score_scale = queries.shape[1] ** (-0.5)
    scores = jnp.dot(queries, key_rows.T, preferred_element_type=jnp.float32) * score_scale
    scores = jnp.where(key_place[None, :] <= query_place[:, None], scores, -1e30)
    row_max = jnp.max(scores, axis=1, keepdims=True)
    raised = jnp.exp(scores - row_max)
    shares = raised / jnp.sum(raised, axis=1, keepdims=True)
    shares_low = shares.astype(jnp.bfloat16)
    outputs = jnp.dot(shares_low, value_rows, preferred_element_type=jnp.float32)
    share_grad = jnp.dot(head_grads, value_rows.T, preferred_element_type=jnp.float32)
    row_delta = jnp.sum(head_grads.astype(jnp.float32) * outputs, axis=1, keepdims=True)
    score_grad = (shares * (share_grad - row_delta) * score_scale).astype(jnp.bfloat16)
    query_grad = jnp.dot(score_grad, key_rows, preferred_element_type=jnp.float32).astype(
        jnp.bfloat16
    )
    key_grad = jnp.dot(score_grad.T, queries, preferred_element_type=jnp.float32)
    value_grad = jnp.dot(shares_low.T, head_grads, preferred_element_type=jnp.float32)
    return (query_grad, key_grad, value_grad)


def per_device(
    layer_input, output_grad, routes, route_gates, query_weight, output_weight, key_values
):
    tokens_here = layer_input.shape[0]
    per_block = query_weight.shape[0]
    expert_count = per_block - 1
    head_width = query_weight.shape[2]
    ctx_count = lax.axis_size("ctx")
    head_count = lax.axis_size("head")
    slot_count = 2 * tokens_here * routes.shape[1] // (expert_count * head_count)
    ctx_index = lax.axis_index("ctx")
    head_index = lax.axis_index("head")
    token_place = (ctx_index * tokens_here + jnp.arange(tokens_here, dtype=jnp.int32)).astype(
        jnp.float32
    )
    key_place = jnp.arange(tokens_here * ctx_count, dtype=jnp.int32).astype(jnp.float32)
    first_id = head_index * expert_count
    tables = slot_table(routes, first_id, expert_count, slot_count)
    tables_low = tables.astype(jnp.bfloat16)
    token_gates = expert_gate(routes, route_gates, first_id, expert_count)
    is_even = head_index % 2 == 0
    own_rows = key_values[0]
    partner_rows = swapped(own_rows, "head", 0)
    key_rows, value_rows = (
        lax.all_gather(jnp.where(is_even, own_rows, partner_rows), "ctx", axis=0, tiled=True),
        lax.all_gather(jnp.where(is_even, partner_rows, own_rows), "ctx", axis=0, tiled=True),
    )
    query_full, output_full = (
        lax.all_gather(query_weight, "ctx", axis=1, tiled=True),
        lax.all_gather(output_weight, "ctx", axis=1, tiled=True),
    )
    picked_input = jnp.einsum(
        "jct,td->jcd", tables_low, layer_input, preferred_element_type=jnp.float32
    ).astype(jnp.bfloat16)
    routed_query = jnp.einsum(
        "jcd,jde->jce", picked_input, query_full[:expert_count], preferred_element_type=jnp.float32
    ).astype(jnp.bfloat16)
    shared_query = jnp.dot(
        layer_input, query_full[expert_count], preferred_element_type=jnp.float32
    ).astype(jnp.bfloat16)
    slot_gate = jnp.einsum("jct,tj->jc", tables, token_gates, precision=PRECISE)
    picked_cotan = jnp.einsum(
        "jct,td->jcd", tables_low, output_grad, preferred_element_type=jnp.float32
    ).astype(jnp.bfloat16)
    routed_sum = jnp.einsum(
        "jcd,jde->jce", picked_cotan, output_full[:expert_count], preferred_element_type=jnp.float32
    )
    shared_sum = jnp.dot(output_grad, output_full[expert_count], preferred_element_type=jnp.float32)
    routed_cotan = (slot_gate[:, :, None] * routed_sum).astype(jnp.bfloat16)
    shared_cotan = shared_sum.astype(jnp.bfloat16)
    routed_place = jnp.einsum("jct,t->jc", tables, token_place, precision=PRECISE)
    queries = jnp.concatenate([routed_query.reshape(-1, head_width), shared_query], axis=0)
    query_place = jnp.concatenate([routed_place.reshape(-1), token_place], axis=0)
    head_grads = jnp.concatenate([routed_cotan.reshape(-1, head_width), shared_cotan], axis=0)
    query_grad, key_grad, value_grad = attend(
        queries, query_place, key_rows, value_rows, key_place, head_grads
    )
    routed_rows = expert_count * slot_count
    routed_qgrad = query_grad[:routed_rows].reshape(expert_count, slot_count, head_width)
    token_qgrad = jnp.einsum(
        "jct,jce->tje", tables_low, routed_qgrad, preferred_element_type=jnp.float32
    ).astype(jnp.bfloat16)
    every_qgrad = jnp.concatenate(
        [token_qgrad, query_grad[routed_rows:].reshape(tokens_here, 1, head_width)], axis=1
    )
    input_term = jnp.einsum(
        "tje,jde->td", every_qgrad, query_full, preferred_element_type=jnp.float32
    )
    input_grad = lax.psum_scatter(input_term, "head", scatter_dimension=1, tiled=True).astype(
        jnp.bfloat16
    )
    outgoing = jnp.where(is_even, value_grad, key_grad)
    incoming = swapped(outgoing.astype(jnp.bfloat16), "head", 0).astype(outgoing.dtype)
    joined_rows = jnp.where(is_even, key_grad, value_grad) + incoming
    kept_rows = lax.psum_scatter(
        joined_rows.astype(jnp.bfloat16), "ctx", scatter_dimension=0, tiled=True
    ).astype(jnp.float32)
    return (input_grad, kept_rows[None])


def solution(mesh):
    in_specs = (
        P("ctx", None),
        P("ctx", None),
        P("ctx", None),
        P("ctx", None),
        P("head", "ctx", None),
        P("head", "ctx", None),
        P("head", "ctx", None),
    )
    out_specs = (P("ctx", "head"), P("head", "ctx", None))
    return jax.shard_map(
        per_device, mesh=mesh, in_specs=in_specs, out_specs=out_specs, check_vma=False
    )
```

profile of v0, /device:TPU:0, one launch (start us, length us, event | category | flops | bytes accessed | tf_op | source)
XLA Modules:
  0.0 364.5 jit_solution(4751156317279246656)
XLA Ops:
  7.2 0.0 copy-start
  7.2 0.0 copy-start.1
  7.2 0.0 copy-start.2
  7.2 0.0 all-gather.5.cloned.1.call-start
  7.2 0.7 all-gather.5.cloned.1.call-update
  7.9 0.0 all-gather.3.cloned.1.call-start
  8.0 0.7 all-gather.3.cloned.1.call-update
  8.7 0.0 reduce-scatter.5.cloned.1.call-start
  8.7 0.0 copy-done
  8.7 3.1 collective-permute-start
  11.8 0.0 copy-done.1
  11.8 0.1 compare_reduce_fusion
  11.9 1.2 reduce-window.6
  13.1 0.1 slice.32
  13.2 0.1 copy.15
  13.4 0.1 copy.16
  13.5 0.1 add_bitcast_fusion
  13.6 0.0 copy-done.2
  13.6 0.1 fusion.61
  13.7 0.4 fusion.40
  14.0 0.3 fusion.38
  14.4 0.0 collective-permute-done
  14.4 5.9 %all_gather.15 = bf16[1024,128]{1,0:T(8,128)(2,1)S(1)} all-gather(bf16[256,128]{1,0:T(8,128)(2,1)S(1)} %get-tuple-element.2), channel_id=1, replica_groups=mesh['ctx'=4,'head'=8] {'ctx'}, dimensions={0}, use_global_device_ids=true | all-gather | bytes 327680 | tf_op jit(solution)/shard_map/all_gather | solution.py:79
  20.3 7.2 %all_gather.13 = bf16[1024,128]{1,0:T(8,128)(2,1)S(1)} all-gather(bf16[256,128]{1,0:T(8,128)(2,1)S(1)} %get-tuple-element.3), channel_id=1, replica_groups=mesh['ctx'=4,'head'=8] {'ctx'}, dimensions={0}, use_global_device_ids=true | all-gather | bytes 327680 | tf_op jit(solution)/shard_map/all_gather | solution.py:78
  27.5 55.9 %all-gather.5.cloned.1.call-done = bf16[5,8192,128]{2,1,0:T(8,128)(2,1)} async-done(((bf16[5,2048,128]{2,1,0:T(8,128)(2,1)}), bf16[5,8192,128]{2,1,0:T(8,128)(2,1)}) %all-gather.5.cloned.1.call-update) | async-done | bytes 10485776 | tf_op jit(solution)/shard_map/all_gather | solution.py:83
  83.4 4.1 %fusion.33 = bf16[256,128]{1,0:T(8,128)(2,1)S(1)} fusion(bf16[256,8192]{1,0:T(8,128)(2,1)} %param.8, bf16[5,8192,128]{2,1,0:T(8,128)(2,1)} %all-gather.5.cloned.1.call-done), kind=kOutput, calls=%fused_computation.28 | convolution fusion | flops 536903680 | bytes 6356992 | tf_op jit(solution)/shard_map/dot_general | solution.py:101
  87.5 0.1 copy.18
  87.6 9.6 %fusion.22 = bf16[4,128,128]{2,1,0:T(8,128)(2,1)S(1)} fusion(bf16[5,8192,128]{2,1,0:T(8,128)(2,1)} %all-gather.5.cloned.1.call-done, bf16[256,8192]{1,0:T(8,128)(2,1)} %param.8, s32[4,256]{1,0:T(4,128)S(1)} %bitcast.78, pred[4,256]{1,0:T(4,128)(4,1)S(1)} %broadcast_compare_fusion, f32[4,128]{1,0:T(4,128)S(1)} %bitcast.84), kind=kOutput, calls=%fused_computation.25 | convolution fusion | flops 3226075136 | bytes 12721152 | tf_op jit(solution)/shard_map/jcd,jde->jce/dot_general | solution.py:98
  97.2 0.1 copy.17
  97.4 58.3 %all-gather.3.cloned.1.call-done = bf16[5,8192,128]{2,1,0:T(8,128)(2,1)} async-done(((bf16[5,2048,128]{2,1,0:T(8,128)(2,1)}), bf16[5,8192,128]{2,1,0:T(8,128)(2,1)}) %all-gather.3.cloned.1.call-update) | async-done | bytes 10485776 | tf_op jit(solution)/shard_map/all_gather | solution.py:82
  155.7 4.1 %fusion.32 = bf16[256,128]{1,0:T(8,128)(2,1)S(1)} fusion(bf16[256,8192]{1,0:T(8,128)(2,1)} %param.7, bf16[5,8192,128]{2,1,0:T(8,128)(2,1)} %all-gather.3.cloned.1.call-done), kind=kOutput, calls=%fused_computation.27 | convolution fusion | flops 536903680 | bytes 6356992 | tf_op jit(solution)/shard_map/dot_general | solution.py:91
  159.8 9.4 %fusion.27 = bf16[4,128,128]{2,1,0:T(8,128)(2,1)S(1)} fusion(bf16[5,8192,128]{2,1,0:T(8,128)(2,1)} %all-gather.3.cloned.1.call-done, bf16[256,8192]{1,0:T(8,128)(2,1)} %param.7, s32[4,256]{1,0:T(4,128)S(1)} %bitcast.79, pred[4,256]{1,0:T(4,128)(4,1)S(1)} %broadcast_compare_fusion), kind=kOutput, calls=%fused_computation.26 | convolution fusion | flops 3226009600 | bytes 12719104 | tf_op jit(solution)/shard_map/jcd,jde->jce/dot_general | solution.py:88
  169.2 0.7 fusion.14
  169.9 0.9 fusion.7
  170.8 0.8 fusion.6
  171.7 0.7 fusion.21
  172.3 0.8 multiply_convert_fusion
  173.2 0.6 convolution_convert_fusion.3
  173.7 0.6 fusion.59
  174.3 0.6 select_convert_fusion
  175.0 1.5 collective-permute-start.1
  176.5 0.3 fusion.15
  176.8 6.7 %collective-permute-done.1 = bf16[1024,128]{1,0:T(8,128)(2,1)S(1)} collective-permute-done((bf16[1024,128]{1,0:T(8,128)(2,1)S(1)}, bf16[1024,128]{1,0:T(8,128)(2,1)S(1)}, u32[]{:S(2)}, u32[]{:S(2)}) %collective-permute-start.1) | collective-permute-done | bytes 262176 | tf_op jit(solution)/shard_map/ppermute | solution.py:12
  183.5 0.8 add_convert_fusion
  184.3 0.0 reduce-scatter.5.cloned.1.call-update
  184.3 0.0 reduce-scatter.3.cloned.1.call-start
  184.4 12.7 %convolution_bitcast_fusion = f32[256,8192]{1,0:T(8,128)} fusion(bf16[5,8192,128]{2,1,0:T(8,128)(2,1)} %all-gather.3.cloned.1.call-done, bf16[256,1,128]{2,0,1:T(8,128)(2,1)S(1)} %slice_bitcast_fusion.8, bf16[256,4,128]{2,0,1:T(8,128)(2,1)S(1)} %fusion.15), kind=kOutput, calls=%fused_computation.2 | convolution fusion | flops 2684518400 | bytes 19202048 | tf_op jit(solution)/shard_map/tje,jde->td/dot_general | solution.py:119
  197.1 0.0 reduce-scatter.3.cloned.1.call-update
  197.1 7.4 %reduce-scatter.5.cloned.1.call-done = bf16[256,128]{1,0:T(8,128)(2,1)} async-done(((bf16[1024,128]{1,0:T(8,128)(2,1)}), bf16[256,128]{1,0:T(8,128)(2,1)}) %reduce-scatter.5.cloned.1.call-update) | async-done | bytes 65552 | tf_op jit(solution)/shard_map/reduce_scatter | solution.py:128
  204.5 1.5 bitcast_convert_fusion
  206.0 149.9 %reduce-scatter.3.cloned.1.call-done = f32[256,1024]{1,0:T(8,128)} async-done(((f32[256,8192]{1,0:T(8,128)}), f32[256,1024]{1,0:T(8,128)}) %reduce-scatter.3.cloned.1.call-update) | async-done | bytes 1048592 | tf_op jit(solution)/shard_map/reduce_scatter | solution.py:122
  355.9 2.1 convert_element_type.91
  (13 shorter events, 0.1 us)
Async XLA Ops:
  7.2 1.6 copy-start
  7.2 4.6 %copy-start.1 = (s32[256,8]{0,1:T(8,128)S(1)}, s32[256,8]{0,1:T(8,128)}, u32[]{:S(2)}) copy-start(s32[256,8]{0,1:T(8,128)} %param.9) | copy-start | bytes 24580
  7.2 6.4 %copy-start.2 = (f32[256,8]{0,1:T(8,128)S(1)}, f32[256,8]{0,1:T(8,128)}, u32[]{:S(2)}) copy-start(f32[256,8]{0,1:T(8,128)} %param.10) | copy-start | bytes 24580
  7.2 76.2 %all-gather.5.cloned.1.call-start = ((), (), s32[]{:S(2)}) async-start(), calls=%async_computation.3 | async-start | bytes 13107200 | tf_op jit(solution)/shard_map/all_gather | solution.py:83
  7.9 147.7 %all-gather.3.cloned.1.call-start = ((), (), s32[]{:S(2)}) async-start(), calls=%async_computation.2 | async-start | bytes 13107200 | tf_op jit(solution)/shard_map/all_gather | solution.py:82
  8.7 195.9 %reduce-scatter.5.cloned.1.call-start = ((), (), s32[]{:S(2)}) async-start(), calls=%async_computation.5 | async-start | bytes 327680 | tf_op jit(solution)/shard_map/reduce_scatter | solution.py:128
  8.7 5.7 %collective-permute-start = (bf16[256,128]{1,0:T(8,128)(2,1)S(1)}, bf16[256,128]{1,0:T(8,128)(2,1)S(1)}, u32[]{:S(2)}, u32[]{:S(2)}) collective-permute-start(bf16[256,128]{1,0:T(8,128)(2,1)S(1)} %bitcast.74), channel_id=1, source_target_pairs={{0,1},{1,0},{2,3},{3,2},{4,5},{5,4},{6,7},{7,6},{8,9},{9,8},{10,11... | collective-permute-start | bytes 196616 | tf_op jit(solution)/shard_map/ppermute | solution.py:12
  175.0 8.5 %collective-permute-start.1 = (bf16[1024,128]{1,0:T(8,128)(2,1)S(1)}, bf16[1024,128]{1,0:T(8,128)(2,1)S(1)}, u32[]{:S(2)}, u32[]{:S(2)}) collective-permute-start(bf16[1024,128]{1,0:T(8,128)(2,1)S(1)} %get-tuple-element.6), channel_id=1, source_target_pairs={{0,1},{1,0},{2,3},{3,2},{4,5},{5,4},{6,7},{7,6},{8,9},{9,8},{10,11... | collective-permute-start | bytes 786440 | tf_op jit(solution)/shard_map/ppermute | solution.py:12
  184.3 171.6 %reduce-scatter.3.cloned.1.call-start = ((), (), s32[]{:S(2)}) async-start(), calls=%async_computation.4 | async-start | bytes 9437184 | tf_op jit(solution)/shard_map/reduce_scatter | solution.py:122
Sparse Core Ops, SparseCore 0:
  9.6 73.7 all-gather.4
  84.9 70.6 all-gather.2
  184.5 20.0 reduce-scatter.4
  208.0 147.8 reduce-scatter.2
where the time goes:
time: 365 us
  waiting for transfers between devices  280 us (77%)
  matrix products  45 us (12%)
  between operations  13.9 us (4%)
  blocking collectives  13.1 us (4%)
  other arithmetic  7.71 us (2%)
  starting transfers between devices  4.74 us (1%)
    reduce_scatter x1, waiting for transfers between devices, per_device(): lax.psum_scatter(input_term, 'head', scatter_dimension=1, tiled=True)  150 us
    all_gather x1, waiting for transfers between devices, per_device(): lax.all_gather(query_weight, 'ctx', axis=1, tiled=True)  58.3 us
    all_gather x1, waiting for transfers between devices, per_device(): lax.all_gather(output_weight, 'ctx', axis=1, tiled=True)  55.9 us
    dot_general x1, matrix products, per_device(): jnp.einsum('tje,jde->td', every_qgrad, query_full, preferred_element_type...  12.7 us
    dot_general x1, matrix products, per_device(): jnp.einsum('jcd,jde->jce', picked_cotan, output_full[:expert_count], pref...  9.65 us
    dot_general x1, matrix products, per_device(): jnp.einsum('jcd,jde->jce', picked_input, query_full[:expert_count], prefe...  9.42 us
    reduce_scatter x1, waiting for transfers between devices, per_device(): lax.psum_scatter(joined_rows.astype(jnp.bfloat16), 'ctx', scatter_dimensi...  7.42 us
  transfers between devices with their start and end apart: 6, of which 5 were waited for; matrix products, arithmetic and copies ran while one was open for 9% of the time, Pallas kernels for 0%

commit v1 on v0

--- a/solution.py
+++ b/solution.py
@@ -79,7 +79,7 @@
         lax.all_gather(jnp.where(is_even, partner_rows, own_rows), "ctx", axis=0, tiled=True),
     )
     query_full, output_full = (
-        lax.all_gather(query_weight, "ctx", axis=1, tiled=True),
+        jnp.concatenate(lax.all_gather(query_weight, "ctx"), axis=1),
         lax.all_gather(output_weight, "ctx", axis=1, tiled=True),
     )
     picked_input = jnp.einsum(

time: 365 us -> 378 us (1.036)
  local copies, waits for them, and re-layouts: 0.55 us -> 21 us
  waiting for transfers between devices: 280 us -> 273 us
    slice x2 -> x4, local copies, waits for them, and re-layouts: 0.18 us -> 11.4 us  [the longest x1 9.12 us: per_device(): query_full[:expert_count]]
    all_gather x0 -> x1, local copies, waits for them, and re-layouts: none -> 9.16 us  [per_device(): lax.all_gather(query_weight, 'ctx')]
    all_gather x1, waiting for transfers between devices: 55.9 us -> 51.9 us  [per_device(): lax.all_gather(output_weight, 'ctx', axis=1, tiled=True)]
  transfers between devices with their start and end apart: 6 -> 6, of which waited for: 5 -> 5; matrix products, arithmetic and copies ran while one was open for 9% -> 10% of each run, Pallas kernels for 0% -> 0%
where the time goes in v1:
time: 378 us; the launch traced here: 377 us
  waiting for transfers between devices  273 us (72%)
  matrix products  44 us (12%)
  local copies, waits for them, and re-layouts  21 us (6%)
  between operations  13.9 us (4%)
  blocking collectives  13.1 us (3%)
  other arithmetic  7.69 us (2%)
  starting transfers between devices  4.74 us (1%)
    reduce_scatter x1, waiting for transfers between devices, per_device(): lax.psum_scatter(input_term, 'head', scatter_dimension=1, tiled=True)  150 us
    all_gather x1, waiting for transfers between devices, per_device(): lax.all_gather(query_weight, 'ctx')  55.9 us
    all_gather x1, waiting for transfers between devices, per_device(): lax.all_gather(output_weight, 'ctx', axis=1, tiled=True)  51.9 us
    dot_general x1, matrix products, per_device(): jnp.einsum('tje,jde->td', every_qgrad, query_full, preferred_element_type...  12.8 us
    dot_general x1, matrix products, per_device(): jnp.einsum('jcd,jde->jce', picked_input, query_full[:expert_count], prefe...  9.41 us
    dot_general x1, matrix products, per_device(): jnp.einsum('jcd,jde->jce', picked_cotan, output_full[:expert_count], pref...  9.22 us
    all_gather x1, local copies, waits for them, and re-layouts, per_device(): lax.all_gather(query_weight, 'ctx')  9.16 us
    slice x1, local copies, waits for them, and re-layouts, per_device(): query_full[:expert_count]  9.12 us
  transfers between devices with their start and end apart: 6, of which 5 were waited for; matrix products, arithmetic and copies ran while one was open for 10% of the time, Pallas kernels for 0%

profile of v1, /device:TPU:0, one launch (start us, length us, event | category | flops | bytes accessed | tf_op | source)
XLA Modules:
  0.0 377.5 jit_solution(9516460742895700307)
XLA Ops:
  7.2 0.0 copy-start
  7.2 0.0 copy-start.1
  7.2 0.0 copy-start.2
  7.2 0.0 all-gather.6.cloned.1.call-start
  7.2 0.7 all-gather.6.cloned.1.call-update
  7.9 0.0 all-gather.4.cloned.1.call-start
  8.0 0.7 all-gather.4.cloned.1.call-update
  8.7 0.0 reduce-scatter.5.cloned.1.call-start
  8.7 0.0 copy-done
  8.7 3.1 collective-permute-start
  11.8 0.0 copy-done.1
  11.8 0.1 compare_reduce_fusion
  11.9 1.2 reduce-window.6
  13.1 0.1 slice.37
  13.2 0.1 copy.23
  13.4 0.1 copy.24
  13.5 0.1 add_bitcast_fusion
  13.6 0.0 copy-done.2
  13.6 0.1 fusion.56
  13.7 0.4 fusion.35
  14.0 0.3 fusion.33
  14.4 0.0 collective-permute-done
  14.4 5.9 %all_gather.19 = bf16[1024,128]{1,0:T(8,128)(2,1)S(1)} all-gather(bf16[256,128]{1,0:T(8,128)(2,1)S(1)} %get-tuple-element.4), channel_id=1, replica_groups=mesh['ctx'=4,'head'=8] {'ctx'}, dimensions={0}, use_global_device_ids=true | all-gather | bytes 327680 | tf_op jit(solution)/shard_map/all_gather | solution.py:79
  20.3 7.2 %all_gather.17 = bf16[1024,128]{1,0:T(8,128)(2,1)S(1)} all-gather(bf16[256,128]{1,0:T(8,128)(2,1)S(1)} %get-tuple-element.5), channel_id=1, replica_groups=mesh['ctx'=4,'head'=8] {'ctx'}, dimensions={0}, use_global_device_ids=true | all-gather | bytes 327680 | tf_op jit(solution)/shard_map/all_gather | solution.py:78
  27.5 55.9 %all-gather.6.cloned.1.call-done = bf16[20,2048,128]{2,1,0:T(8,128)(2,1)} async-done(((bf16[5,2048,128]{2,1,0:T(8,128)(2,1)}), bf16[20,2048,128]{2,1,0:T(8,128)(2,1)}) %all-gather.6.cloned.1.call-update) | async-done | bytes 10485776 | tf_op jit(solution)/shard_map/all_gather | solution.py:82
  83.4 9.2 %copy.43 = bf16[4,5,2048,128]{3,2,0,1:T(8,128)(2,1)} copy(bf16[4,5,2048,128]{3,2,1,0:T(8,128)(2,1)} %bitcast.78) | data formatting | bytes 20971520 | tf_op jit(solution)/shard_map/all_gather | solution.py:82
  92.5 2.1 slice.39
  94.6 9.1 %slice.38 = bf16[4,4,2048,128]{3,2,1,0:T(8,128)(2,1)} slice(bf16[5,4,2048,128]{3,2,1,0:T(8,128)(2,1)} %bitcast.76), slice={[0:4], [0:4], [0:2048], [0:128]} | slice | bytes 16777216 | tf_op jit(solution)/shard_map/slice | solution.py:89
  103.7 51.9 %all-gather.4.cloned.1.call-done = bf16[5,8192,128]{2,1,0:T(8,128)(2,1)} async-done(((bf16[5,2048,128]{2,1,0:T(8,128)(2,1)}), bf16[5,8192,128]{2,1,0:T(8,128)(2,1)}) %all-gather.4.cloned.1.call-update) | async-done | bytes 10485776 | tf_op jit(solution)/shard_map/all_gather | solution.py:83
  155.7 4.1 %fusion.28 = bf16[256,128]{1,0:T(8,128)(2,1)S(1)} fusion(bf16[256,8192]{1,0:T(8,128)(2,1)} %param.8, bf16[5,8192,128]{2,1,0:T(8,128)(2,1)} %all-gather.4.cloned.1.call-done), kind=kOutput, calls=%fused_computation.24 | convolution fusion | flops 536903680 | bytes 6356992 | tf_op jit(solution)/shard_map/dot_general | solution.py:101
  159.8 0.1 copy.27
  159.9 9.2 %fusion.20 = bf16[4,128,128]{2,1,0:T(8,128)(2,1)S(1)} fusion(bf16[5,8192,128]{2,1,0:T(8,128)(2,1)} %all-gather.4.cloned.1.call-done, bf16[256,8192]{1,0:T(8,128)(2,1)} %param.8, s32[4,256]{1,0:T(4,128)S(1)} %bitcast.89, pred[4,256]{1,0:T(4,128)(4,1)S(1)} %broadcast_compare_fusion, f32[4,128]{1,0:T(4,128)S(1)} %bitcast.95), kind=kOutput, calls=%fused_computation.22 | convolution fusion | flops 3226075136 | bytes 12721152 | tf_op jit(solution)/shard_map/jcd,jde->jce/dot_general | solution.py:98
  169.1 0.1 copy.26
  169.2 3.4 convolution_convert_fusion.4
  172.7 9.4 %fusion.25 = bf16[4,128,128]{2,1,0:T(8,128)(2,1)S(1)} fusion(bf16[4,8192,128]{2,1,0:T(8,128)(2,1)} %bitcast.80, bf16[256,8192]{1,0:T(8,128)(2,1)} %param.7, s32[4,256]{1,0:T(4,128)S(1)} %bitcast.90, pred[4,256]{1,0:T(4,128)(4,1)S(1)} %broadcast_compare_fusion), kind=kOutput, calls=%fused_computation.23 | convolution fusion | flops 3226009600 | bytes 12719104 | tf_op jit(solution)/shard_map/jcd,jde->jce/dot_general | solution.py:88
  182.1 0.7 fusion.9
  182.8 0.9 fusion.5
  183.7 0.8 fusion.4
  184.6 0.7 fusion.19
  185.2 0.8 multiply_convert_fusion
  186.1 0.6 convolution_convert_fusion.3
  186.7 0.6 fusion.54
  187.3 0.6 select_convert_fusion
  187.9 1.5 collective-permute-start.1
  189.4 0.1 copy.29
  189.6 0.3 fusion.13
  189.8 6.6 %collective-permute-done.1 = bf16[1024,128]{1,0:T(8,128)(2,1)S(1)} collective-permute-done((bf16[1024,128]{1,0:T(8,128)(2,1)S(1)}, bf16[1024,128]{1,0:T(8,128)(2,1)S(1)}, u32[]{:S(2)}, u32[]{:S(2)}) %collective-permute-start.1) | collective-permute-done | bytes 262176 | tf_op jit(solution)/shard_map/ppermute | solution.py:12
  196.4 0.8 add_convert_fusion
  197.2 0.0 reduce-scatter.5.cloned.1.call-update
  197.2 0.0 reduce-scatter.3.cloned.1.call-start
  197.3 12.8 %convolution_bitcast_fusion = f32[256,8192]{1,0:T(8,128)} fusion(bf16[5,8192,128]{2,1,0:T(8,128)(2,1)} %bitcast.77, bf16[256,1,128]{0,2,1:T(8,128)(2,1)S(1)} %copy.29, bf16[256,4,128]{0,2,1:T(8,128)(2,1)S(1)} %fusion.13), kind=kOutput, calls=%fused_computation.2 | convolution fusion | flops 2684518400 | bytes 19202048 | tf_op jit(solution)/shard_map/tje,jde->td/dot_general | solution.py:119
  210.1 0.0 reduce-scatter.3.cloned.1.call-update
  210.1 7.3 %reduce-scatter.5.cloned.1.call-done = bf16[256,128]{1,0:T(8,128)(2,1)} async-done(((bf16[1024,128]{1,0:T(8,128)(2,1)}), bf16[256,128]{1,0:T(8,128)(2,1)}) %reduce-scatter.5.cloned.1.call-update) | async-done | bytes 65552 | tf_op jit(solution)/shard_map/reduce_scatter | solution.py:128
  217.4 1.5 bitcast_convert_fusion
  218.9 149.9 %reduce-scatter.3.cloned.1.call-done = f32[256,1024]{1,0:T(8,128)} async-done(((f32[256,8192]{1,0:T(8,128)}), f32[256,1024]{1,0:T(8,128)}) %reduce-scatter.3.cloned.1.call-update) | async-done | bytes 1048592 | tf_op jit(solution)/shard_map/reduce_scatter | solution.py:122
  368.8 2.1 convert_element_type.91
  (13 shorter events, 0.1 us)
Async XLA Ops:
  7.2 1.6 copy-start
  7.2 4.6 %copy-start.1 = (s32[256,8]{0,1:T(8,128)S(1)}, s32[256,8]{0,1:T(8,128)}, u32[]{:S(2)}) copy-start(s32[256,8]{0,1:T(8,128)} %param.9) | copy-start | bytes 24580
  7.2 6.4 %copy-start.2 = (f32[256,8]{0,1:T(8,128)S(1)}, f32[256,8]{0,1:T(8,128)}, u32[]{:S(2)}) copy-start(f32[256,8]{0,1:T(8,128)} %param.10) | copy-start | bytes 24580
  7.2 76.2 %all-gather.6.cloned.1.call-start = ((), (), s32[]{:S(2)}) async-start(), calls=%async_computation.5 | async-start | bytes 13107200 | tf_op jit(solution)/shard_map/all_gather | solution.py:82
  7.9 147.7 %all-gather.4.cloned.1.call-start = ((), (), s32[]{:S(2)}) async-start(), calls=%async_computation.2 | async-start | bytes 13107200 | tf_op jit(solution)/shard_map/all_gather | solution.py:83
  8.7 208.8 %reduce-scatter.5.cloned.1.call-start = ((), (), s32[]{:S(2)}) async-start(), calls=%async_computation.4 | async-start | bytes 327680 | tf_op jit(solution)/shard_map/reduce_scatter | solution.py:128
  8.7 5.7 %collective-permute-start = (bf16[256,128]{1,0:T(8,128)(2,1)S(1)}, bf16[256,128]{1,0:T(8,128)(2,1)S(1)}, u32[]{:S(2)}, u32[]{:S(2)}) collective-permute-start(bf16[256,128]{1,0:T(8,128)(2,1)S(1)} %bitcast.85), channel_id=1, source_target_pairs={{0,1},{1,0},{2,3},{3,2},{4,5},{5,4},{6,7},{7,6},{8,9},{9,8},{10,11... | collective-permute-start | bytes 196616 | tf_op jit(solution)/shard_map/ppermute | solution.py:12
  187.9 8.5 %collective-permute-start.1 = (bf16[1024,128]{1,0:T(8,128)(2,1)S(1)}, bf16[1024,128]{1,0:T(8,128)(2,1)S(1)}, u32[]{:S(2)}, u32[]{:S(2)}) collective-permute-start(bf16[1024,128]{1,0:T(8,128)(2,1)S(1)} %get-tuple-element.8), channel_id=1, source_target_pairs={{0,1},{1,0},{2,3},{3,2},{4,5},{5,4},{6,7},{7,6},{8,9},{9,8},{10,11... | collective-permute-start | bytes 786440 | tf_op jit(solution)/shard_map/ppermute | solution.py:12
  197.2 171.6 %reduce-scatter.3.cloned.1.call-start = ((), (), s32[]{:S(2)}) async-start(), calls=%async_computation.3 | async-start | bytes 9437184 | tf_op jit(solution)/shard_map/reduce_scatter | solution.py:122
Sparse Core Ops, SparseCore 0:
  9.6 73.7 all-gather.5
  84.9 70.6 all-gather.3
  197.3 20.0 reduce-scatter.4
  220.9 147.8 reduce-scatter.2
